TPU v7x, 32 devices: a whole 2x2x4 slice. The times are simulated.
32 devices in a mesh: tm: 8 (over z, core), dp: 4 (over y, x).
Axes of the slice: x: 2, y: 2, z: 4, core: 2. Of those that a mesh axis runs over, the one named last changes fastest.
Arguments:
- encoded: bfloat16 [512, 80, 1024], P('dp', 'tm'), may hold values from -6 to 6
- queries: bfloat16 [512, 32, 1024], P(('dp', 'tm')), may hold values from -200 to 200
- cotangent: bfloat16 [512, 32, 1024], P(('dp', 'tm')), may hold values from -0.08886719 to 0.08886719
- lengths: int32 [512], P(('dp', 'tm')), may hold values from 2 to 80
- key_weight: bfloat16 [1024, 1024], replicated, may hold values from -0.1875 to 0.1875
- value_weight: bfloat16 [1024, 1024], replicated, may hold values from -0.1875 to 0.1875
Outputs:
- context: bfloat16 [512, 32, 1024], P(('dp', 'tm'))
- key_grad: float32 [1024, 1024], replicated
- value_grad: float32 [1024, 1024], replicated
Inputs may be any that keep to these rules, and one draw needn't show every extreme that they name: Sequence b attends only to source positions below lengths[b].
All inputs are finite; a program needn't handle non-finite values.
Results may differ from a plain program's by a relative error of at most 0.0069.
Values may be sent and summed in bfloat16 or wider, within the bound.
A program may use at most 128 MiB of HBM per device.

v0:
```python
import math
import jax
import jax.numpy as jnp
from jax import lax
from jax.sharding import PartitionSpec as P


def attend(queries, key_rows, value_rows, lengths, cotangent):
    score_scale = 1.0 / math.sqrt(queries.shape[-1])
    scores = (
        jnp.einsum("btd,bsd->bts", queries, key_rows, preferred_element_type=jnp.float32)
        * score_scale
    )
    positions = jnp.arange(key_rows.shape[1], dtype=jnp.int32)
    in_range = positions[None, None, :] < lengths[:, None, None]
    scores = jnp.where(in_range, scores, -1e30)
    row_max = jnp.max(scores, axis=-1, keepdims=True)
    weights = jnp.exp(scores - row_max)
    probabilities = weights / jnp.sum(weights, axis=-1, keepdims=True)
    probs_low = probabilities.astype(jnp.bfloat16)
    context = jnp.einsum(
        "bts,bsd->btd", probs_low, value_rows, preferred_element_type=jnp.float32
    ).astype(jnp.bfloat16)
    grad_probs = jnp.einsum(
        "btd,bsd->bts", cotangent, value_rows, preferred_element_type=jnp.float32
    )
    grad_scores = probabilities * (
        grad_probs - jnp.sum(probabilities * grad_probs, axis=-1, keepdims=True)
    )
    grad_low = grad_scores.astype(jnp.bfloat16)
    grad_values = jnp.einsum(
        "bts,btd->bsd", probs_low, cotangent, preferred_element_type=jnp.float32
    ).astype(jnp.bfloat16)
    grad_keys = (
        jnp.einsum("bts,btd->bsd", grad_low, queries, preferred_element_type=jnp.float32)
        * score_scale
    ).astype(jnp.bfloat16)
    return (context, grad_keys, grad_values)


def project(flattened, weight_matrix, shape):
    return (
        jnp.dot(flattened, weight_matrix, preferred_element_type=jnp.float32)
        .astype(jnp.bfloat16)
        .reshape(shape)
    )


def weight_term(flattened, gradient):
    model_width = flattened.shape[1]
    return lax.dot_general(
        flattened,
        gradient.reshape(-1, model_width),
        (((0,), (0,)), ((), ())),
        preferred_element_type=jnp.float32,
    )


def body(encoded, queries, cotangent, lengths, key_weight, value_weight):
    model_width = encoded.shape[2]
    regrouped = lax.all_to_all(encoded, "tm", split_axis=0, concat_axis=1, tiled=True)
    flattened = regrouped.reshape(-1, model_width)
    key_rows = project(flattened, key_weight, regrouped.shape)
    value_rows = project(flattened, value_weight, regrouped.shape)
    context, grad_keys, grad_values = attend(queries, key_rows, value_rows, lengths, cotangent)
    key_grad = weight_term(flattened, grad_keys)
    value_grad = weight_term(flattened, grad_values)
    key_grad, value_grad = lax.psum((key_grad, value_grad), ("tm", "dp"))
    return (context, key_grad, value_grad)


def solution(mesh):
    return jax.shard_map(
        body,
        mesh=mesh,
        in_specs=(
            P("dp", "tm", None),
            P(("dp", "tm"), None, None),
            P(("dp", "tm"), None, None),
            P(("dp", "tm")),
            P(),
            P(),
        ),
        out_specs=(P(("dp", "tm"), None, None), P(), P()),
        check_vma=False,
    )
```

profile of v0, /device:TPU:0, one launch (start us, length us, event | category | flops | bytes accessed | tf_op | source)
XLA Modules:
  0.0 355.5 jit_solution(7292842336370048144)
XLA Ops:
  7.2 0.0 copy-start
  7.2 5.5 %copy.14 = bf16[128,10,1024]{2,1,0:T(8,128)(2,1)} copy(bf16[128,10,1024]{2,0,1:T(8,128)(2,1)} %param.6) | data formatting | bytes 5242880 | tf_op args[0]
  12.7 0.0 copy-start.5
  12.7 6.5 %all-to-all-start = ((bf16[128,10,1024]{2,1,0:T(8,128)(2,1)}), bf16[128,10,1024]{2,1,0:T(8,128)(2,1)}, u32[]{:S(2)}, u32[]{:S(2)}) async-start(bf16[128,10,1024]{2,1,0:T(8,128)(2,1)} %copy.14), calls=%async_computation | async-start | bytes 8388608 | tf_op jit(solution)/shard_map/all_to_all | solution.py:61
  19.2 0.0 all-reduce.3.cloned.1.call-start
  19.2 0.0 copy-done.5
  19.3 0.1 iota_compare_fusion
  19.3 94.0 %all-to-all-done = bf16[128,10,1024]{2,1,0:T(8,128)(2,1)} async-done(((bf16[128,10,1024]{2,1,0:T(8,128)(2,1)}), bf16[128,10,1024]{2,1,0:T(8,128)(2,1)}, u32[]{:S(2)}, u32[]{:S(2)}) %all-to-all-start) | async-done | bytes 2621472 | tf_op jit(solution)/shard_map/all_to_all | solution.py:61
  113.3 5.0 %copy.19 = bf16[8,16,10,1024]{3,2,0,1:T(8,128)(2,1)} copy(bf16[8,16,10,1024]{3,2,1,0:T(8,128)(2,1)} %bitcast) | data formatting | bytes 5242880 | tf_op jit(solution)/shard_map/all_to_all | solution.py:61
  118.3 6.1 %reshape.46 = bf16[1280,1024]{1,0:T(8,128)(2,1)} reshape(bf16[16,8,10,1024]{3,2,1,0:T(8,128)(2,1)} %bitcast.35) | data formatting | bytes 5242880 | tf_op jit(solution)/shard_map/reshape | solution.py:62
  124.5 0.0 copy-done
  124.5 0.0 copy-start.3
  124.5 0.0 copy-start.6
  124.5 6.1 %convolution_convert_fusion = bf16[1280,1024]{1,0:T(8,128)(2,1)} fusion(bf16[1280,1024]{1,0:T(8,128)(2,1)} %reshape.46, bf16[1024,1024]{1,0:T(8,128)(2,1)S(1)} %copy-done), kind=kOutput, calls=%fused_computation.3 | convolution fusion | flops 2685665280 | bytes 7340032 | tf_op jit(solution)/shard_map/dot_general | solution.py:43
  130.6 0.0 copy-done.3
  130.6 0.0 copy-done.6
  130.6 3.1 convolution_convert_fusion.1
  133.7 0.0 copy-done.1
  133.7 0.8 fusion.4
  134.6 0.9 fusion.8
  135.4 4.6 %convolution_convert_fusion.2 = bf16[16,80,1024]{2,1,0:T(8,128)(2,1)} fusion(bf16[16,32,1024]{2,1,0:T(8,128)(2,1)} %param.8, f32[16,32]{1,0:T(8,128)S(1)} %get-tuple-element.14, f32[16,32,80]{2,1,0:T(8,128)S(1)} %fusion.4), kind=kOutput, calls=%fused_computation.7 | convolution fusion | flops 85320272 | bytes 3835904 | tf_op jit(solution)/shard_map/bts,btd->bsd/dot_general | solution.py:31
  140.0 3.6 %multiply_reduce_fusion = (f32[16,32]{1,0:T(8,128)S(1)}, f32[16,32,80]{2,1,0:T(8,128)}) fusion(f32[16,32,80]{2,1,0:T(8,128)} %get-tuple-element.15, f32[16,32]{1,0:T(8,128)S(1)} %get-tuple-element.14, bf16[16,80,1024]{2,1,0:T(8,128)(2,1)} %bitcast.36, bf16[16,32,1024]{2,1,0:T(8,128)(2,1)} %param.8), kind=kOutput, calls=%fused_computation.16 | convolution fusion | flops 84008448 | bytes 4001792 | tf_op jit(solution)/shard_map/btd,bsd->bts/dot_general | solution.py:24
  143.6 4.1 %multiply_convert_fusion = bf16[16,80,1024]{2,1,0:T(8,128)(2,1)} fusion(bf16[16,32,1024]{2,1,0:T(8,128)(2,1)S(1)} %copy-done.1, f32[16,32,80]{2,1,0:T(8,128)} %get-tuple-element.17, f32[16,32]{1,0:T(8,128)S(1)} %get-tuple-element.16, f32[16,32]{1,0:T(8,128)S(1)} %get-tuple-element.14, f32[16,32,80]{2,1,0:T(8,128)S(1)} %fusion.4), kind=kOutput, calls=%fused_computation.1 | convolution fusion | flops 86712912 | bytes 4001792 | tf_op jit(solution)/shard_map/bts,btd->bsd/dot_general | solution.py:35
  147.8 7.6 %convolution_bitcast_fusion.1 = f32[1024,1024]{0,1:T(8,128)} fusion(bf16[1280,1024]{1,0:T(8,128)(2,1)} %bitcast.40, bf16[1280,1024]{1,0:T(8,128)(2,1)} %reshape.46), kind=kOutput, calls=%fused_computation.6 | convolution fusion | flops 2684354560 | bytes 9437184 | tf_op jit(solution)/shard_map/dot_general | solution.py:51
  155.4 0.0 copy-done.2
  155.4 0.0 copy-done.4
  155.4 4.4 %convolution_bitcast_fusion = f32[1024,1024]{0,1:T(8,128)} fusion(bf16[1280,1024]{1,0:T(8,128)(2,1)S(1)} %bitcast.38, bf16[1280,1024]{1,0:T(8,128)(2,1)S(1)} %copy-done.4), kind=kOutput, calls=%fused_computation.5 | convolution fusion | flops 2684354560 | bytes 9437184 | tf_op jit(solution)/shard_map/dot_general | solution.py:51
  159.8 0.0 all-reduce.3.cloned.1.call-update
  159.9 3.8 %convolution_convert_fusion.3 = bf16[16,32,1024]{2,1,0:T(8,128)(2,1)} fusion(bf16[16,80,1024]{2,1,0:T(8,128)(2,1)} %bitcast.37, f32[16,32]{1,0:T(8,128)S(1)} %get-tuple-element.14, f32[16,32,80]{2,1,0:T(8,128)S(1)} %fusion.4), kind=kOutput, calls=%fused_computation.8 | convolution fusion | flops 84533840 | bytes 3835904 | tf_op jit(solution)/shard_map/bts,bsd->btd/dot_general | solution.py:21
  163.7 174.3 %all-reduce.3.cloned.1.call-done = (f32[1024,1024]{0,1:T(8,128)}, f32[1024,1024]{0,1:T(8,128)}) async-done(((f32[1024,1024]{0,1:T(8,128)}, f32[1024,1024]{0,1:T(8,128)}), (f32[1024,1024]{0,1:T(8,128)}, f32[1024,1024]{0,1:T(8,128)})) %all-reduce.3.cloned.1.call-update) | async-done | bytes 8388624 | tf_op jit(solution)/shard_map/psum | solution.py:68
  338.0 5.3 %copy.16 = f32[1024,1024]{1,0:T(8,128)} copy(f32[1024,1024]{0,1:T(8,128)} %get-tuple-element.12) | data formatting | bytes 8388608
  343.4 5.3 %copy.17 = f32[1024,1024]{1,0:T(8,128)} copy(f32[1024,1024]{0,1:T(8,128)} %get-tuple-element.13) | data formatting | bytes 8388608
  (3 shorter events, 0.0 us)
Async XLA Ops:
  7.2 117.3 %copy-start = (bf16[1024,1024]{1,0:T(8,128)(2,1)S(1)}, bf16[1024,1024]{1,0:T(8,128)(2,1)}, u32[]{:S(2)}) copy-start(bf16[1024,1024]{1,0:T(8,128)(2,1)} %param.11) | copy-start | bytes 6291460
  12.7 6.5 %copy-start.5 = (s32[16]{0:T(128)S(1)}, s32[16]{0:T(128)}, u32[]{:S(2)}) copy-start(s32[16]{0:T(128)} %param.9) | copy-start | bytes 196
  12.7 100.6 %all-to-all-start = ((bf16[128,10,1024]{2,1,0:T(8,128)(2,1)}), bf16[128,10,1024]{2,1,0:T(8,128)(2,1)}, u32[]{:S(2)}, u32[]{:S(2)}) async-start(bf16[128,10,1024]{2,1,0:T(8,128)(2,1)} %copy.14), calls=%async_computation | async-start | bytes 8388608 | tf_op jit(solution)/shard_map/all_to_all | solution.py:61
  19.2 318.8 %all-reduce.3.cloned.1.call-start = ((), (), s32[]{:S(2)}) async-start(), calls=%async_computation.1 | async-start | bytes 16777216 | tf_op jit(solution)/shard_map/psum | solution.py:68
  124.5 6.1 %copy-start.3 = (bf16[1280,1024]{1,0:T(8,128)(2,1)S(1)}, bf16[1280,1024]{1,0:T(8,128)(2,1)}, u32[]{:S(2)}) copy-start(bf16[1280,1024]{1,0:T(8,128)(2,1)} %reshape.46) | copy-start | bytes 7864324
  124.5 6.1 %copy-start.6 = (bf16[1024,1024]{1,0:T(8,128)(2,1)S(1)}, bf16[1024,1024]{1,0:T(8,128)(2,1)}, u32[]{:S(2)}) copy-start(bf16[1024,1024]{1,0:T(8,128)(2,1)} %param.10) | copy-start | bytes 6291460
  130.6 3.1 copy-start.1
  147.8 7.6 %copy-start.2 = (bf16[16,80,1024]{2,1,0:T(8,128)(2,1)S(1)}, bf16[16,80,1024]{2,1,0:T(8,128)(2,1)}, u32[]{:S(2)}) copy-start(bf16[16,80,1024]{2,1,0:T(8,128)(2,1)} %convolution_convert_fusion.2) | copy-start | bytes 7864324
  147.8 7.6 %copy-start.4 = (bf16[1280,1024]{1,0:T(8,128)(2,1)S(1)}, bf16[1280,1024]{1,0:T(8,128)(2,1)}, u32[]{:S(2)}) copy-start(bf16[1280,1024]{1,0:T(8,128)(2,1)} %reshape.46) | copy-start | bytes 7864324
Sparse Core Ops, SparseCore 0:
  160.0 177.9 all-reduce.2
where the time goes:
time: 356 us
  waiting for transfers between devices  268 us (75%)
  matrix products  38.3 us (11%)
  local copies, waits for them, and re-layouts  27.4 us (8%)
  between operations  14.1 us (4%)
  starting transfers between devices  6.52 us (2%)
    psum x1, waiting for transfers between devices, body(): key_grad, value_grad = lax.psum((key_grad, value_grad), ('tm', 'dp'))  174 us
    all_to_all x1, waiting for transfers between devices, body(): lax.all_to_all(encoded, 'tm', split_axis=0, concat_axis=1, tiled=True)  94 us
    unnamed x17, local copies, waits for them, and re-layouts  16.2 us
    dot_general x2, matrix products, weight_term(): lax.dot_general(flattened, gradient.reshape(-1, model_width), (((0,), (0,...  12.1 us
    dot_general x2, matrix products, project(): jnp.dot(flattened, weight_matrix, preferred_element_type=jnp.float32)  9.23 us
  transfers between devices with their start and end apart: 2, of which 2 were waited for; matrix products, arithmetic and copies ran while one was open for 1% of the time, Pallas kernels for 0%

commit v1 on v0

--- a/solution.py
+++ b/solution.py
@@ -65,7 +65,7 @@
     context, grad_keys, grad_values = attend(queries, key_rows, value_rows, lengths, cotangent)
     key_grad = weight_term(flattened, grad_keys)
     value_grad = weight_term(flattened, grad_values)
-    key_grad, value_grad = lax.psum((key_grad, value_grad), ("tm", "dp"))
+    key_grad, value_grad = lax.psum(lax.psum((key_grad, value_grad), "dp"), "tm")
     return (context, key_grad, value_grad)
 
 

time: 356 us -> 527 us (1.48)
  waiting for transfers between devices: 268 us -> 440 us
    psum x1 -> x2, waiting for transfers between devices: 174 us -> 346 us  [the longest x1 175 us: body(): lax.psum(lax.psum((key_grad, value_grad), 'dp'), 'tm')]
    unnamed x17 -> x21, local copies, waits for them, and re-layouts: 16.2 us -> 16.4 us
  transfers between devices with their start and end apart: 2 -> 3, of which waited for: 2 -> 3; matrix products, arithmetic and copies ran while one was open for 1% -> 1% of each run, Pallas kernels for 0% -> 0%
where the time goes in v1:
time: 527 us; the launch traced here: 526 us
  waiting for transfers between devices  440 us (83%)
  matrix products  35.2 us (7%)
  local copies, waits for them, and re-layouts  27.6 us (5%)
  between operations  14.1 us (3%)
  starting transfers between devices  6.56 us (1%)
    psum x1, waiting for transfers between devices, body(): lax.psum(lax.psum((key_grad, value_grad), 'dp'), 'tm')  175 us
    psum x1, waiting for transfers between devices, body(): lax.psum((key_grad, value_grad), 'dp')  171 us
    all_to_all x1, waiting for transfers between devices, body(): lax.all_to_all(encoded, 'tm', split_axis=0, concat_axis=1, tiled=True)  94 us
    unnamed x21, local copies, waits for them, and re-layouts  16.4 us
    dot_general x2, matrix products, weight_term(): lax.dot_general(flattened, gradient.reshape(-1, model_width), (((0,), (0,...  12.1 us
  transfers between devices with their start and end apart: 3, of which 3 were waited for; matrix products, arithmetic and copies ran while one was open for 1% of the time, Pallas kernels for 0%

profile of v1, /device:TPU:0, one launch (start us, length us, event | category | flops | bytes accessed | tf_op | source)
XLA Modules:
  0.0 526.2 jit_solution(5877260115512305339)
XLA Ops:
  7.2 0.0 copy-start
  7.2 5.5 %copy.14 = bf16[128,10,1024]{2,1,0:T(8,128)(2,1)} copy(bf16[128,10,1024]{2,0,1:T(8,128)(2,1)} %param.6) | data formatting | bytes 5242880 | tf_op args[0]
  12.7 6.5 %all-to-all-start = ((bf16[128,10,1024]{2,1,0:T(8,128)(2,1)}), bf16[128,10,1024]{2,1,0:T(8,128)(2,1)}, u32[]{:S(2)}, u32[]{:S(2)}) async-start(bf16[128,10,1024]{2,1,0:T(8,128)(2,1)} %copy.14), calls=%async_computation | async-start | bytes 8388608 | tf_op jit(solution)/shard_map/all_to_all | solution.py:61
  19.2 0.0 all-reduce.7.cloned.1.call-start
  19.2 0.0 copy-done.7
  19.3 0.1 iota_compare_fusion
  19.3 94.0 %all-to-all-done = bf16[128,10,1024]{2,1,0:T(8,128)(2,1)} async-done(((bf16[128,10,1024]{2,1,0:T(8,128)(2,1)}), bf16[128,10,1024]{2,1,0:T(8,128)(2,1)}, u32[]{:S(2)}, u32[]{:S(2)}) %all-to-all-start) | async-done | bytes 2621472 | tf_op jit(solution)/shard_map/all_to_all | solution.py:61
  113.3 5.0 copy.19
  118.3 6.1 %reshape.46 = bf16[1280,1024]{1,0:T(8,128)(2,1)} reshape(bf16[16,8,10,1024]{3,2,1,0:T(8,128)(2,1)} %bitcast.35) | data formatting | bytes 5242880 | tf_op jit(solution)/shard_map/reshape | solution.py:62
  124.5 0.0 copy-done
  124.5 6.2 %convolution_convert_fusion = bf16[1280,1024]{1,0:T(8,128)(2,1)} fusion(bf16[1280,1024]{1,0:T(8,128)(2,1)} %reshape.46, bf16[1024,1024]{1,0:T(8,128)(2,1)S(1)} %copy-done), kind=kOutput, calls=%fused_computation.3 | convolution fusion | flops 2685665280 | bytes 7340032 | tf_op jit(solution)/shard_map/dot_general | solution.py:43
  130.6 0.0 copy-done.4
  130.7 0.0 copy-done.8
  130.7 3.1 convolution_convert_fusion.1
  133.8 0.0 copy-start.6
  133.8 0.0 copy-done.2
  133.8 0.8 fusion.4
  134.6 2.8 fusion.8
  137.4 0.0 copy-done.6
  137.4 3.4 convolution_convert_fusion.2
  140.8 2.6 multiply_reduce_fusion
  143.4 3.2 multiply_convert_fusion
  146.6 7.6 %convolution_bitcast_fusion.1 = f32[1024,1024]{0,1:T(8,128)} fusion(bf16[1280,1024]{1,0:T(8,128)(2,1)} %bitcast.40, bf16[1280,1024]{1,0:T(8,128)(2,1)} %reshape.46), kind=kOutput, calls=%fused_computation.6 | convolution fusion | flops 2684354560 | bytes 9437184 | tf_op jit(solution)/shard_map/dot_general | solution.py:51
  154.2 4.4 convolution_bitcast_fusion
  158.7 0.0 all-reduce.7.cloned.1.call-update
  158.7 0.0 all-reduce.5.cloned.1.call-start
  158.8 171.1 %all-reduce.7.cloned.1.call-done = (f32[1024,1024]{0,1:T(8,128)}, f32[1024,1024]{0,1:T(8,128)}) async-done(((f32[1024,1024]{0,1:T(8,128)}, f32[1024,1024]{0,1:T(8,128)}), (f32[1024,1024]{0,1:T(8,128)}, f32[1024,1024]{0,1:T(8,128)})) %all-reduce.7.cloned.1.call-update) | async-done | bytes 8388624 | tf_op jit(solution)/shard_map/psum | solution.py:68
  329.8 0.0 all-reduce.5.cloned.1.call-update
  329.9 3.8 convolution_convert_fusion.3
  333.7 174.8 %all-reduce.5.cloned.1.call-done = (f32[1024,1024]{0,1:T(8,128)}, f32[1024,1024]{0,1:T(8,128)}) async-done(((f32[1024,1024]{0,1:T(8,128)}, f32[1024,1024]{0,1:T(8,128)}), (f32[1024,1024]{0,1:T(8,128)}, f32[1024,1024]{0,1:T(8,128)})) %all-reduce.5.cloned.1.call-update) | async-done | bytes 8388624 | tf_op jit(solution)/shard_map/psum | solution.py:68
  508.5 5.3 %copy.16 = f32[1024,1024]{1,0:T(8,128)} copy(f32[1024,1024]{0,1:T(8,128)} %get-tuple-element.12) | data formatting | bytes 8388608
  513.9 5.5 %copy.17 = f32[1024,1024]{1,0:T(8,128)} copy(f32[1024,1024]{0,1:T(8,128)} %get-tuple-element.13) | data formatting | bytes 8388608
  (10 shorter events, 0.0 us)
Async XLA Ops:
  7.2 117.3 %copy-start = (bf16[1024,1024]{1,0:T(8,128)(2,1)S(1)}, bf16[1024,1024]{1,0:T(8,128)(2,1)}, u32[]{:S(2)}) copy-start(bf16[1024,1024]{1,0:T(8,128)(2,1)} %param.11) | copy-start | bytes 6291460
  12.7 6.5 %copy-start.7 = (s32[16]{0:T(128)S(1)}, s32[16]{0:T(128)}, u32[]{:S(2)}) copy-start(s32[16]{0:T(128)} %param.9) | copy-start | bytes 196
  12.7 100.6 %all-to-all-start = ((bf16[128,10,1024]{2,1,0:T(8,128)(2,1)}), bf16[128,10,1024]{2,1,0:T(8,128)(2,1)}, u32[]{:S(2)}, u32[]{:S(2)}) async-start(bf16[128,10,1024]{2,1,0:T(8,128)(2,1)} %copy.14), calls=%async_computation | async-start | bytes 8388608 | tf_op jit(solution)/shard_map/all_to_all | solution.py:61
  19.2 310.6 %all-reduce.7.cloned.1.call-start = ((), (), s32[]{:S(2)}) async-start(), calls=%async_computation.2 | async-start | bytes 16777216 | tf_op jit(solution)/shard_map/psum | solution.py:68
  124.5 6.2 %copy-start.4 = (bf16[1280,1024]{1,0:T(8,128)(2,1)S(1)}, bf16[1280,1024]{1,0:T(8,128)(2,1)}, u32[]{:S(2)}) copy-start(bf16[1280,1024]{1,0:T(8,128)(2,1)} %reshape.46) | copy-start | bytes 7864324
  124.5 6.2 %copy-start.8 = (bf16[1024,1024]{1,0:T(8,128)(2,1)S(1)}, bf16[1024,1024]{1,0:T(8,128)(2,1)}, u32[]{:S(2)}) copy-start(bf16[1024,1024]{1,0:T(8,128)(2,1)} %param.10) | copy-start | bytes 6291460
  130.7 3.1 copy-start.2
  133.8 3.6 copy-start.6
  146.6 7.6 %copy-start.3 = (bf16[16,80,1024]{2,1,0:T(8,128)(2,1)S(1)}, bf16[16,80,1024]{2,1,0:T(8,128)(2,1)}, u32[]{:S(2)}) copy-start(bf16[16,80,1024]{2,1,0:T(8,128)(2,1)} %convolution_convert_fusion.2) | copy-start | bytes 7864324
  146.6 7.6 %copy-start.5 = (bf16[1280,1024]{1,0:T(8,128)(2,1)S(1)}, bf16[1280,1024]{1,0:T(8,128)(2,1)}, u32[]{:S(2)}) copy-start(bf16[1280,1024]{1,0:T(8,128)(2,1)} %reshape.46) | copy-start | bytes 7864324
  158.7 349.8 %all-reduce.5.cloned.1.call-start = ((), (), s32[]{:S(2)}) async-start(), calls=%async_computation.1 | async-start | bytes 16777216 | tf_op jit(solution)/shard_map/psum | solution.py:68
  513.9 5.5 %copy-start.1 = (bf16[1024,1024]{1,0:T(8,128)(2,1)S(1)}, bf16[1024,1024]{1,0:T(8,128)(2,1)}, u32[]{:S(2)}) copy-start(bf16[1024,1024]{1,0:T(8,128)(2,1)} %param.11) | copy-start | bytes 6291460
Sparse Core Ops, SparseCore 0:
  158.8 170.9 all-reduce.6
  332.2 176.2 all-reduce.4
